TPU v7x, 32 devices: a whole 2x2x4 slice. The times are simulated.
32 devices in a mesh: gx: 4 (over y, x), gy: 4 (over z), gz: 2 (over core).
Axes of the slice: x: 2, y: 2, z: 4, core: 2. Of those that a mesh axis runs over, the one named last changes fastest.
Arguments:
- rhs_coarse: bfloat16 [32, 32, 128], P('gx'), may hold values from -24 to 24
- rhs_mid: bfloat16 [64, 64, 256], P('gx', 'gy'), may hold values from -24 to 24
- rhs_fine: bfloat16 [128, 128, 512], P('gx', 'gy', 'gz'), may hold values from -24 to 24
- occupied_coarse: int32 [4, 4, 16], P('gx'), may hold values 0 or 1
- occupied_mid: int32 [8, 8, 32], P('gx', 'gy'), may hold values 0 or 1
- occupied_fine: int32 [16, 16, 64], P('gx', 'gy', 'gz'), may hold values 0 or 1
- screen_weight: float32 [3], replicated, may hold values from 0.2 to 2
Outputs:
- solution_coarse: float32 [32, 32, 128], P('gx')
- solution_mid: float32 [64, 64, 256], P('gx', 'gy')
- solution_fine: float32 [128, 128, 512], P('gx', 'gy', 'gz')
All inputs are finite; a program needn't handle non-finite values. No bound on the sum of `occupied_coarse` or of `occupied_mid` or of `occupied_fine` on one device may be relied on, other than what follows from the above.
Results may differ from a plain program's by a relative error of at most 0.0003.
Values sent between devices are 32-bit elements; how exact they have to be, the bound alone decides.
A program may use at most 128 MiB of HBM per device.

v0:
```python
import jax
import jax.numpy as jnp
from jax import lax
from jax.sharding import PartitionSpec as P

CG_ITERS = 2


def extended_2(shard, sides, width):
    for axis, dim in sides:
        count, length = (lax.axis_size(axis), shard.shape[dim])
        up = [(i, (i + 1) % count) for i in range(count - 1)]
        down = [(j, i) for i, j in up]
        last = lax.slice_in_dim(shard, length - width, length, axis=dim)
        first = lax.slice_in_dim(shard, 0, width, axis=dim)
        before = lax.ppermute(last, axis, up)
        after = lax.ppermute(first, axis, down)
        shard = jnp.concatenate([before, shard, after], axis=dim)
    return shard


def alternate(even_cells, odd_cells, dim_index):
    stacked = jnp.stack([even_cells, odd_cells], axis=dim_index + 1)
    new_shape = list(even_cells.shape)
    new_shape[dim_index] = new_shape[dim_index] * 2
    return stacked.reshape(new_shape)


def prolong_axis(padded, dim_index):
    length = padded.shape[dim_index]
    below_cells = lax.slice_in_dim(padded, 0, length - 2, axis=dim_index)
    middle = lax.slice_in_dim(padded, 1, length - 1, axis=dim_index)
    above_cells = lax.slice_in_dim(padded, 2, length, axis=dim_index)
    refined = alternate(
        0.75 * middle + 0.25 * below_cells, 0.75 * middle + 0.25 * above_cells, dim_index
    )
    first_rim = 0.75 * lax.slice_in_dim(padded, 0, 1, axis=dim_index) + 0.25 * lax.slice_in_dim(
        padded, 1, 2, axis=dim_index
    )
    last_rim = 0.75 * lax.slice_in_dim(
        padded, length - 1, length, axis=dim_index
    ) + 0.25 * lax.slice_in_dim(padded, length - 2, length - 1, axis=dim_index)
    refined = jnp.concatenate([first_rim, refined, last_rim], axis=dim_index)
    return refined


def screening(occupied, weight, brick_side):
    brick_flags = occupied.astype(jnp.float32)
    brick_shape = occupied.shape
    spread = jnp.broadcast_to(
        brick_flags[:, None, :, None, :, None],
        (brick_shape[0], brick_side, brick_shape[1], brick_side, brick_shape[2], brick_side),
    )
    cell_flags = spread.reshape(
        brick_shape[0] * brick_side, brick_shape[1] * brick_side, brick_shape[2] * brick_side
    )
    return weight * (0.25 + cell_flags)


def stencil(padded, screen):
    centre = padded[1:-1, 1:-1, 1:-1]
    beside = padded[2:, 1:-1, 1:-1] + padded[:-2, 1:-1, 1:-1]
    beside = beside + padded[1:-1, 2:, 1:-1] + padded[1:-1, :-2, 1:-1]
    beside = beside + padded[1:-1, 1:-1, 2:] + padded[1:-1, 1:-1, :-2]
    return (6.0 + screen) * centre - beside


def padded_field(values, depth_level):
    if depth_level == 0:
        padded = extended_2(values, (("gx", 0),), 1)
        return jnp.pad(padded, ((0, 0), (1, 1), (1, 1)))
    if depth_level == 1:
        padded = extended_2(values, (("gx", 0), ("gy", 1)), 1)
        return jnp.pad(padded, ((0, 0), (0, 0), (1, 1)))
    return extended_2(values, (("gx", 0), ("gy", 1), ("gz", 2)), 1)


def level_sum(values, depth_level):
    if depth_level == 0:
        return lax.psum((values[0],), "gx")
    if depth_level == 1:
        return lax.psum((values[0],), ("gx", "gy"))
    return lax.psum((values[0],), ("gx", "gy", "gz"))


def clear_rim(extended, dim_index, edges):
    extent = extended.shape[dim_index]
    view_shape = [1, 1, 1]
    view_shape[dim_index] = extent
    position = lax.broadcasted_iota(jnp.int32, tuple(view_shape), dim_index)
    low_out, high_out = edges
    cleared = jnp.logical_or(
        jnp.logical_and(position == 0, low_out), jnp.logical_and(position == extent - 1, high_out)
    )
    return jnp.where(cleared, jnp.float32(0.0), extended)


def refine_guess(coarse, fine_shape, depth_level):
    x_edges = (lax.axis_index("gx") == 0, lax.axis_index("gx") == lax.axis_size("gx") - 1)
    y_edges = (lax.axis_index("gy") == 0, lax.axis_index("gy") == lax.axis_size("gy") - 1)
    if depth_level == 1:
        padded = extended_2(coarse, (("gx", 0),), 1)
        padded = jnp.pad(padded, ((0, 0), (1, 1), (1, 1)))
        block_rows = fine_shape[1] // 2
        block_start = lax.axis_index("gy") * block_rows
        padded = lax.dynamic_slice_in_dim(padded, block_start, block_rows + 2, 1)
        edges = (x_edges, y_edges, (True, True))
    else:
        padded = extended_2(coarse, (("gx", 0), ("gy", 1)), 1)
        padded = jnp.pad(padded, ((0, 0), (0, 0), (1, 1)))
        block_rows = fine_shape[2] // 2
        block_start = lax.axis_index("gz") * block_rows
        padded = lax.dynamic_slice_in_dim(padded, block_start, block_rows + 2, 2)
        z_edges = (lax.axis_index("gz") == 0, lax.axis_index("gz") == lax.axis_size("gz") - 1)
        edges = (x_edges, y_edges, z_edges)
    extended = padded
    for dim_index in range(3):
        extended = prolong_axis(extended, dim_index)
    for dim_index in range(3):
        extended = clear_rim(extended, dim_index, edges[dim_index])
    return (extended[1:-1, 1:-1, 1:-1], extended)


def cg_solve(right_side, guess, padded_guess, screen, depth_level):
    target = right_side.astype(jnp.float32)
    if guess is None:
        iterate = jnp.zeros_like(target)
        residual = target
    else:
        iterate = guess
        residual = target - stencil(padded_guess, screen)
    direction = residual
    (norm_now,) = level_sum((jnp.sum(residual * residual),), depth_level)
    for turn_index in range(CG_ITERS):
        image = stencil(padded_field(direction, depth_level), screen)
        (curvature,) = level_sum((jnp.sum(direction * image),), depth_level)
        step_size = norm_now / curvature
        iterate = iterate + step_size * direction
        residual = residual - step_size * image
        if turn_index + 1 < CG_ITERS:
            (norm_next,) = level_sum((jnp.sum(residual * residual),), depth_level)
            direction = residual + norm_next / norm_now * direction
            norm_now = norm_next
    return iterate


def shards(
    rhs_coarse, rhs_mid, rhs_fine, occupied_coarse, occupied_mid, occupied_fine, screen_weight
):
    screen_coarse = screening(
        occupied_coarse, screen_weight[0], rhs_coarse.shape[0] // occupied_coarse.shape[0]
    )
    screen_mid = screening(
        occupied_mid, screen_weight[1], rhs_mid.shape[0] // occupied_mid.shape[0]
    )
    screen_fine = screening(
        occupied_fine, screen_weight[2], rhs_fine.shape[0] // occupied_fine.shape[0]
    )
    solution_coarse = cg_solve(rhs_coarse, None, None, screen_coarse, 0)
    guess_mid, padded_mid = refine_guess(solution_coarse, rhs_mid.shape, 1)
    solution_mid = cg_solve(rhs_mid, guess_mid, padded_mid, screen_mid, 1)
    guess_fine, padded_fine = refine_guess(solution_mid, rhs_fine.shape, 2)
    solution_fine = cg_solve(rhs_fine, guess_fine, padded_fine, screen_fine, 2)
    return (solution_coarse, solution_mid, solution_fine)


def solution(mesh):
    in_specs = (
        P("gx", None, None),
        P("gx", "gy", None),
        P("gx", "gy", "gz"),
        P("gx", None, None),
        P("gx", "gy", None),
        P("gx", "gy", "gz"),
        P(),
    )
    out_specs = (P("gx", None, None), P("gx", "gy", None), P("gx", "gy", "gz"))
    return jax.shard_map(shards, mesh=mesh, in_specs=in_specs, out_specs=out_specs, check_vma=False)
```

profile of v0, /device:TPU:0, one launch (start us, length us, event | category | flops | bytes accessed | tf_op | source)
XLA Modules:
  0.0 495.4 jit_solution(4594889696543994090)
XLA Ops:
  1.6 4.9 collective-permute-start.1
  13.3 11.7 %all-reduce.8 = (f32[]{:T(128)}, f32[]{:T(128)}) all-reduce(f32[]{:T(128)} %get-tuple-element.20, f32[]{:T(128)} %get-tuple-element.19), channel_id=1, replica_groups=mesh['gx'=4,'gy'=4,'gz'=2] {'gx'}, use_global_device_ids=true, to_apply=%region_1.0 | all-reduce | flops 2 | bytes 16 | tf_op jit(solution)/shard_map/psum | solution.py:80
  26.9 9.5 %psum.86 = f32[]{:T(128)} all-reduce(f32[]{:T(128)} %multiply_reduce_fusion.6), channel_id=1, replica_groups=mesh['gx'=4,'gy'=4,'gz'=2] {'gx'}, use_global_device_ids=true, to_apply=%region_5.6 | all-reduce | flops 1 | bytes 8 | tf_op jit(solution)/shard_map/psum | solution.py:80
  41.7 4.2 collective-permute-done.2
  47.1 10.5 %psum.87 = f32[]{:T(128)} all-reduce(f32[]{:T(128)} %fusion.85), channel_id=1, replica_groups=mesh['gx'=4,'gy'=4,'gz'=2] {'gx'}, use_global_device_ids=true, to_apply=%region_7.8 | all-reduce | flops 1 | bytes 8 | tf_op jit(solution)/shard_map/psum | solution.py:80
  60.3 4.5 collective-permute-start.4
  67.4 4.0 add.347
  81.8 4.2 collective-permute-done.6
  91.0 4.2 collective-permute-done.8
  96.4 39.0 %all-reduce.7 = (f32[]{:T(128)}, f32[]{:T(128)}) all-reduce(f32[]{:T(128)} %get-tuple-element.18, f32[]{:T(128)} %get-tuple-element.17), channel_id=1, replica_groups=mesh['gx'=4,'gy'=4,'gz'=2] {'gx','gy'}, use_global_device_ids=true, to_apply=%region_9.10 | all-reduce | flops 2 | bytes 16 | tf_op jit(solution)/shard_map/psum | solution.py:82
  137.5 37.8 %psum.90 = f32[]{:T(128)} all-reduce(f32[]{:T(128)} %multiply_reduce_fusion.3), channel_id=1, replica_groups=mesh['gx'=4,'gy'=4,'gz'=2] {'gx','gy'}, use_global_device_ids=true, to_apply=%region_13.14 | all-reduce | flops 1 | bytes 8 | tf_op jit(solution)/shard_map/psum | solution.py:82
  179.3 8.0 %collective-permute-done.10 = f32[1,16,256]{2,1,0:T(8,128)S(1)} collective-permute-done((f32[1,16,256]{2,1,0:T(8,128)S(1)}, f32[1,16,256]{2,1,0:T(8,128)S(1)}, u32[]{:S(2)}, u32[]{:S(2)}) %collective-permute-start.10) | collective-permute-done | bytes 16416 | tf_op jit(solution)/shard_map/ppermute | solution.py:17
  187.4 3.8 collective-permute-start.13
  192.6 4.2 collective-permute-done.12
  198.0 37.4 %psum.91 = f32[]{:T(128)} all-reduce(f32[]{:T(128)} %fusion.42), channel_id=1, replica_groups=mesh['gx'=4,'gy'=4,'gz'=2] {'gx','gy'}, use_global_device_ids=true, to_apply=%region_15.16 | all-reduce | flops 1 | bytes 8 | tf_op jit(solution)/shard_map/psum | solution.py:82
  240.2 5.0 %collective-permute-done.15 = f32[1,16,256]{2,1,0:T(8,128)S(1)} collective-permute-done((f32[1,16,256]{2,1,0:T(8,128)S(1)}, f32[1,16,256]{2,1,0:T(8,128)S(1)}, u32[]{:S(2)}, u32[]{:S(2)}) %collective-permute-start.15) | collective-permute-done | bytes 16416 | tf_op jit(solution)/shard_map/ppermute | solution.py:17
  245.2 3.8 collective-permute-start.16
  250.5 8.0 %broadcast_in_dim.95 = f32[4,8,4,8,32,8]{5,4,3,2,1,0:T(8,128)} broadcast(f32[4,4,32]{2,1,0:T(4,128)S(1)} %multiply_add_fusion.6), dimensions={0,2,4} | broadcast | bytes 1050624 | tf_op jit(solution)/shard_map/broadcast_in_dim | solution.py:50
  258.4 13.5 %add.382 = f32[32,32,256]{2,1,0:T(8,128)} reshape(f32[4,8,4,8,32,8]{5,4,3,2,1,0:T(8,128)} %broadcast_in_dim.95) | data formatting | bytes 2097152 | tf_op jit(solution)/shard_map/add | solution.py:65
  278.2 4.5 copy.136
  289.7 4.8 collective-permute-start.19
  296.1 4.2 collective-permute-done.18
  300.4 4.5 collective-permute-start.21
  306.6 4.2 collective-permute-done.20
  322.2 6.1 %multiply_reduce_fusion.1 = (f32[]{:T(128)}, f32[]{:T(128)}, f32[32,32,256]{2,1,0:T(8,128)}) fusion(f32[32,32,256]{2,1,0:T(8,128)S(1)} %fusion.17, f32[34,1,256]{2,1,0:T(1,128)S(1)} %collective-permute-done.20, f32[1,32,256]{2,1,0:T(8,128)S(1)} %collective-permute-done.18, f32[1,32,256]{2,1,0:T(8,128)S(1)} %collective-permute-done.19, ...), kind=kLoop, calls=%fused_computation.76 | loop fusion | flops 7602174 | bytes 3290152 | tf_op jit(solution)/shard_map/reduce_sum | solution.py:136
  328.2 37.9 %all-reduce.6 = (f32[]{:T(128)}, f32[]{:T(128)}) all-reduce(f32[]{:T(128)} %get-tuple-element.16, f32[]{:T(128)} %get-tuple-element.15), channel_id=1, replica_groups=mesh['gx'=4,'gy'=4,'gz'=2] {'gx','gy','gz'}, use_global_device_ids=true, to_apply=%region_17.18 | all-reduce | flops 2 | bytes 16 | tf_op jit(solution)/shard_map/psum | solution.py:83
  369.7 41.3 %psum.94 = f32[]{:T(128)} all-reduce(f32[]{:T(128)} %multiply_reduce_fusion), channel_id=1, replica_groups=mesh['gx'=4,'gy'=4,'gz'=2] {'gx','gy','gz'}, use_global_device_ids=true, to_apply=%region_21.22 | all-reduce | flops 1 | bytes 8 | tf_op jit(solution)/shard_map/psum | solution.py:83
  413.8 4.2 collective-permute-start.25
  419.6 4.2 collective-permute-done.24
  427.4 4.2 collective-permute-done.26
  442.8 8.0 %fusion.5 = f32[]{:T(128)} fusion(f32[32,32,256]{2,1,0:T(8,128)} %copy-done, f32[34,34,1]{2,1,0:T(8,128)} %copy.145, f32[34,1,256]{2,1,0:T(1,128)S(1)} %collective-permute-done.26, f32[34,1,256]{2,1,0:T(1,128)S(1)} %collective-permute-done.27, f32[1,32,256]{2,1,0:T(8,128)S(1)} %collective-permute-done.24, f32[1,32,256]{2,1,0:T(8,128)S(1)} %collective-permute-done.25, ...), kind=kLoop, calls=%fused_computation.19 | loop fusion | flops 7077887 | bytes 2241572 | tf_op jit(solution)/shard_map/reduce_sum | solution.py:136
  451.5 39.9 %psum.95 = f32[]{:T(128)} all-reduce(f32[]{:T(128)} %fusion.5), channel_id=1, replica_groups=mesh['gx'=4,'gy'=4,'gz'=2] {'gx','gy','gz'}, use_global_device_ids=true, to_apply=%region_23.24 | all-reduce | flops 1 | bytes 8 | tf_op jit(solution)/shard_map/psum | solution.py:83
  (160 shorter events, 95.4 us)
Async XLA Ops:
  1.6 10.5 %collective-permute-start.1 = (f32[1,32,128]{2,0,1:T(1,128)S(1)}, f32[1,32,128]{2,0,1:T(1,128)S(1)}, u32[]{:S(2)}, u32[]{:S(2)}) collective-permute-start(f32[1,32,128]{2,0,1:T(1,128)S(1)} %get-tuple-element.82), channel_id=1, source_target_pairs={{0,8},{8,16},{16,24},{1,9},{9,17},{17,25},{2,10},{10,18},{18,26},{... | collective-permute-start | bytes 49160 | tf_op jit(solution)/shard_map/ppermute | solution.py:16
  6.5 5.7 %collective-permute-start = (f32[1,32,128]{2,0,1:T(1,128)S(1)}, f32[1,32,128]{2,0,1:T(1,128)S(1)}, u32[]{:S(2)}, u32[]{:S(2)}) collective-permute-start(f32[1,32,128]{2,0,1:T(1,128)S(1)} %get-tuple-element.83), channel_id=1, source_target_pairs={{8,0},{16,8},{24,16},{9,1},{17,9},{25,17},{10,2},{18,10},{26,18},{... | collective-permute-start | bytes 49160 | tf_op jit(solution)/shard_map/ppermute | solution.py:17
  37.8 3.9 collective-permute-start.3
  40.3 5.6 %collective-permute-start.2 = (f32[1,32,128]{2,0,1:T(1,128)S(1)}, f32[1,32,128]{2,0,1:T(1,128)S(1)}, u32[]{:S(2)}, u32[]{:S(2)}) collective-permute-start(f32[1,32,128]{2,0,1:T(1,128)S(1)} %get-tuple-element.81), channel_id=1, source_target_pairs={{8,0},{16,8},{24,16},{9,1},{17,9},{25,17},{10,2},{18,10},{26,18},{... | collective-permute-start | bytes 49160 | tf_op jit(solution)/shard_map/ppermute | solution.py:17
  59.0 12.4 %collective-permute-start.5 = (f32[1,32,128]{2,0,1:T(1,128)S(1)}, f32[1,32,128]{2,0,1:T(1,128)S(1)}, u32[]{:S(2)}, u32[]{:S(2)}) collective-permute-start(f32[1,32,128]{2,0,1:T(1,128)S(1)} %get-tuple-element.78), channel_id=1, source_target_pairs={{8,0},{16,8},{24,16},{9,1},{17,9},{25,17},{10,2},{18,10},{26,18},{... | collective-permute-start | bytes 49160 | tf_op jit(solution)/shard_map/ppermute | solution.py:17
  60.3 11.2 %collective-permute-start.4 = (f32[1,32,128]{2,0,1:T(1,128)S(1)}, f32[1,32,128]{2,0,1:T(1,128)S(1)}, u32[]{:S(2)}, u32[]{:S(2)}) collective-permute-start(f32[1,32,128]{2,0,1:T(1,128)S(1)} %get-tuple-element.79), channel_id=1, source_target_pairs={{0,8},{8,16},{16,24},{1,9},{9,17},{17,25},{2,10},{10,18},{18,26},{... | collective-permute-start | bytes 49160 | tf_op jit(solution)/shard_map/ppermute | solution.py:16
  77.6 4.2 collective-permute-start.7
  80.4 5.6 %collective-permute-start.6 = (f32[1,16,256]{2,1,0:T(8,128)S(1)}, f32[1,16,256]{2,1,0:T(8,128)S(1)}, u32[]{:S(2)}, u32[]{:S(2)}) collective-permute-start(f32[1,16,256]{2,1,0:T(8,128)S(1)} %get-tuple-element.69), channel_id=1, source_target_pairs={{8,0},{16,8},{24,16},{9,1},{17,9},{25,17},{10,2},{18,10},{26,18},{... | collective-permute-start | bytes 49160 | tf_op jit(solution)/shard_map/ppermute | solution.py:17
  86.1 4.9 collective-permute-start.9
  89.5 5.7 %collective-permute-start.8 = (f32[18,1,256]{2,1,0:T(1,128)S(1)}, f32[18,1,256]{2,1,0:T(1,128)S(1)}, u32[]{:S(2)}, u32[]{:S(2)}) collective-permute-start(f32[18,1,256]{2,1,0:T(1,128)S(1)} %get-tuple-element.63), channel_id=1, source_target_pairs={{2,0},{4,2},{6,4},{3,1},{5,3},{7,5},{10,8},{12,10},{14,12},{11,9},... | collective-permute-start | bytes 55304 | tf_op jit(solution)/shard_map/ppermute | solution.py:17
  176.6 2.7 collective-permute-start.11
  177.9 9.4 %collective-permute-start.10 = (f32[1,16,256]{2,1,0:T(8,128)S(1)}, f32[1,16,256]{2,1,0:T(8,128)S(1)}, u32[]{:S(2)}, u32[]{:S(2)}) collective-permute-start(f32[1,16,256]{2,1,0:T(8,128)S(1)} %get-tuple-element.67), channel_id=1, source_target_pairs={{8,0},{16,8},{24,16},{9,1},{17,9},{25,17},{10,2},{18,10},{26,18},{... | collective-permute-start | bytes 49160 | tf_op jit(solution)/shard_map/ppermute | solution.py:17
  187.4 5.2 %collective-permute-start.13 = (f32[18,1,256]{2,1,0:T(1,128)S(1)}, f32[18,1,256]{2,1,0:T(1,128)S(1)}, u32[]{:S(2)}, u32[]{:S(2)}) collective-permute-start(f32[18,1,256]{2,1,0:T(1,128)S(1)} %get-tuple-element.60), channel_id=1, source_target_pairs={{0,2},{2,4},{4,6},{1,3},{3,5},{5,7},{8,10},{10,12},{12,14},{9,11},... | collective-permute-start | bytes 55304 | tf_op jit(solution)/shard_map/ppermute | solution.py:16
  191.1 48.4 %copy-start.8 = (s32[4,4,32]{2,1,0:T(4,128)S(1)}, s32[4,4,32]{2,1,0:T(4,128)}, u32[]{:S(2)}) copy-start(s32[4,4,32]{2,1,0:T(4,128)} %param.12) | copy-start | bytes 6148
  191.1 5.7 %collective-permute-start.12 = (f32[18,1,256]{2,1,0:T(1,128)S(1)}, f32[18,1,256]{2,1,0:T(1,128)S(1)}, u32[]{:S(2)}, u32[]{:S(2)}) collective-permute-start(f32[18,1,256]{2,1,0:T(1,128)S(1)} %get-tuple-element.61), channel_id=1, source_target_pairs={{2,0},{4,2},{6,4},{3,1},{5,3},{7,5},{10,8},{12,10},{14,12},{11,9},... | collective-permute-start | bytes 55304 | tf_op jit(solution)/shard_map/ppermute | solution.py:17
  236.9 35.1 %copy-start.2 = (f32[16,16,256]{2,1,0:T(8,128)}, f32[16,16,256]{2,1,0:T(8,128)S(1)}, u32[]{:S(2)}) copy-start(f32[16,16,256]{2,1,0:T(8,128)S(1)} %multiply_add_fusion.2) | copy-start | bytes 786436
  236.9 3.3 collective-permute-start.14
  238.2 6.9 %collective-permute-start.15 = (f32[1,16,256]{2,1,0:T(8,128)S(1)}, f32[1,16,256]{2,1,0:T(8,128)S(1)}, u32[]{:S(2)}, u32[]{:S(2)}) collective-permute-start(f32[1,16,256]{2,1,0:T(8,128)S(1)} %get-tuple-element.65), channel_id=1, source_target_pairs={{8,0},{16,8},{24,16},{9,1},{17,9},{25,17},{10,2},{18,10},{26,18},{... | collective-permute-start | bytes 49160 | tf_op jit(solution)/shard_map/ppermute | solution.py:17
  245.2 26.8 %collective-permute-start.16 = (f32[18,1,256]{2,1,0:T(1,128)S(1)}, f32[18,1,256]{2,1,0:T(1,128)S(1)}, u32[]{:S(2)}, u32[]{:S(2)}) collective-permute-start(f32[18,1,256]{2,1,0:T(1,128)S(1)} %get-tuple-element.58), channel_id=1, source_target_pairs={{0,2},{2,4},{4,6},{1,3},{3,5},{5,7},{8,10},{10,12},{12,14},{9,11},... | collective-permute-start | bytes 55304 | tf_op jit(solution)/shard_map/ppermute | solution.py:16
  249.0 23.0 %collective-permute-start.17 = (f32[18,1,256]{2,1,0:T(1,128)S(1)}, f32[18,1,256]{2,1,0:T(1,128)S(1)}, u32[]{:S(2)}, u32[]{:S(2)}) collective-permute-start(f32[18,1,256]{2,1,0:T(1,128)S(1)} %get-tuple-element.59), channel_id=1, source_target_pairs={{2,0},{4,2},{6,4},{3,1},{5,3},{7,5},{10,8},{12,10},{14,12},{11,9},... | collective-permute-start | bytes 55304 | tf_op jit(solution)/shard_map/ppermute | solution.py:17
  289.7 6.4 %collective-permute-start.19 = (f32[1,32,256]{2,1,0:T(8,128)S(1)}, f32[1,32,256]{2,1,0:T(8,128)S(1)}, u32[]{:S(2)}, u32[]{:S(2)}) collective-permute-start(f32[1,32,256]{2,1,0:T(8,128)S(1)} %get-tuple-element.44), channel_id=1, source_target_pairs={{0,8},{8,16},{16,24},{1,9},{9,17},{17,25},{2,10},{10,18},{18,26},{... | collective-permute-start | bytes 98312 | tf_op jit(solution)/shard_map/ppermute | solution.py:16
  294.6 5.8 %collective-permute-start.18 = (f32[1,32,256]{2,1,0:T(8,128)S(1)}, f32[1,32,256]{2,1,0:T(8,128)S(1)}, u32[]{:S(2)}, u32[]{:S(2)}) collective-permute-start(f32[1,32,256]{2,1,0:T(8,128)S(1)} %get-tuple-element.45), channel_id=1, source_target_pairs={{8,0},{16,8},{24,16},{9,1},{17,9},{25,17},{10,2},{18,10},{26,18},{... | collective-permute-start | bytes 98312 | tf_op jit(solution)/shard_map/ppermute | solution.py:17
  300.4 6.2 %collective-permute-start.21 = (f32[34,1,256]{2,1,0:T(1,128)S(1)}, f32[34,1,256]{2,1,0:T(1,128)S(1)}, u32[]{:S(2)}, u32[]{:S(2)}) collective-permute-start(f32[34,1,256]{2,1,0:T(1,128)S(1)} %get-tuple-element.40), channel_id=1, source_target_pairs={{0,2},{2,4},{4,6},{1,3},{3,5},{5,7},{8,10},{10,12},{12,14},{9,11},... | collective-permute-start | bytes 104456 | tf_op jit(solution)/shard_map/ppermute | solution.py:16
  305.0 5.8 %collective-permute-start.20 = (f32[34,1,256]{2,1,0:T(1,128)S(1)}, f32[34,1,256]{2,1,0:T(1,128)S(1)}, u32[]{:S(2)}, u32[]{:S(2)}) collective-permute-start(f32[34,1,256]{2,1,0:T(1,128)S(1)} %get-tuple-element.41), channel_id=1, source_target_pairs={{2,0},{4,2},{6,4},{3,1},{5,3},{7,5},{10,8},{12,10},{14,12},{11,9},... | collective-permute-start | bytes 104456 | tf_op jit(solution)/shard_map/ppermute | solution.py:17
  313.7 6.0 %collective-permute-start.22 = (f32[34,34,1]{1,2,0:T(1,128)S(1)}, f32[34,34,1]{1,2,0:T(1,128)S(1)}, u32[]{:S(2)}, u32[]{:S(2)}) collective-permute-start(f32[34,34,1]{1,2,0:T(1,128)S(1)} %copy.147), channel_id=1, source_target_pairs={{1,0},{3,2},{5,4},{7,6},{9,8},{11,10},{13,12},{15,14},{17,16},{19,... | collective-permute-start | bytes 13880 | tf_op jit(solution)/shard_map/ppermute | solution.py:17
  316.5 4.5 collective-permute-start.23
  413.8 5.8 %collective-permute-start.25 = (f32[1,32,256]{2,1,0:T(8,128)S(1)}, f32[1,32,256]{2,1,0:T(8,128)S(1)}, u32[]{:S(2)}, u32[]{:S(2)}) collective-permute-start(f32[1,32,256]{2,1,0:T(8,128)S(1)} %get-tuple-element.42), channel_id=1, source_target_pairs={{0,8},{8,16},{16,24},{1,9},{9,17},{17,25},{2,10},{10,18},{18,26},{... | collective-permute-start | bytes 98312 | tf_op jit(solution)/shard_map/ppermute | solution.py:16
  418.0 5.8 %collective-permute-start.24 = (f32[1,32,256]{2,1,0:T(8,128)S(1)}, f32[1,32,256]{2,1,0:T(8,128)S(1)}, u32[]{:S(2)}, u32[]{:S(2)}) collective-permute-start(f32[1,32,256]{2,1,0:T(8,128)S(1)} %get-tuple-element.43), channel_id=1, source_target_pairs={{8,0},{16,8},{24,16},{9,1},{17,9},{25,17},{10,2},{18,10},{26,18},{... | collective-permute-start | bytes 98312 | tf_op jit(solution)/shard_map/ppermute | solution.py:17
  423.9 3.5 collective-permute-start.27
  425.8 5.8 %collective-permute-start.26 = (f32[34,1,256]{2,1,0:T(1,128)S(1)}, f32[34,1,256]{2,1,0:T(1,128)S(1)}, u32[]{:S(2)}, u32[]{:S(2)}) collective-permute-start(f32[34,1,256]{2,1,0:T(1,128)S(1)} %get-tuple-element.39), channel_id=1, source_target_pairs={{2,0},{4,2},{6,4},{3,1},{5,3},{7,5},{10,8},{12,10},{14,12},{11,9},... | collective-permute-start | bytes 104456 | tf_op jit(solution)/shard_map/ppermute | solution.py:17
  434.6 5.8 %collective-permute-start.28 = (f32[34,34,1]{1,2,0:T(1,128)S(1)}, f32[34,34,1]{1,2,0:T(1,128)S(1)}, u32[]{:S(2)}, u32[]{:S(2)}) collective-permute-start(f32[34,34,1]{1,2,0:T(1,128)S(1)} %copy.149), channel_id=1, source_target_pairs={{1,0},{3,2},{5,4},{7,6},{9,8},{11,10},{13,12},{15,14},{17,16},{19,... | collective-permute-start | bytes 13880 | tf_op jit(solution)/shard_map/ppermute | solution.py:17
  437.3 4.2 collective-permute-start.29
  (7 other events, 56.0 us)
where the time goes:
time: 497 us; the launch traced here: 495 us
  blocking collectives  265 us (53%)
  starting transfers between devices  69.6 us (14%)
  local copies, waits for them, and re-layouts  58.1 us (12%)
  waiting for transfers between devices  48.5 us (10%)
  other arithmetic  40.6 us (8%)
  between operations  13.6 us (3%)
    psum x3, blocking collectives, level_sum(): return lax.psum((values[0],), ('gx', 'gy', 'gz'))  119 us
    psum x3, blocking collectives, level_sum(): return lax.psum((values[0],), ('gx', 'gy'))  114 us
    ppermute x15, starting transfers between devices, extended_2(): before = lax.ppermute(last, axis, up)  50.1 us
    ppermute x15, waiting for transfers between devices, extended_2(): after = lax.ppermute(first, axis, down)  46.7 us
    psum x3, blocking collectives, level_sum(): return lax.psum((values[0],), 'gx')  31.7 us
    ppermute x15, starting transfers between devices, extended_2(): after = lax.ppermute(first, axis, down)  19.5 us
    add x3, local copies, waits for them, and re-layouts, stencil(): return (6.0 + screen) * centre - beside  17.7 us
    reduce_sum x6, other arithmetic, cg_solve(): curvature, = level_sum((jnp.sum(direction * image),), depth_level)  17.4 us
  transfers between devices with their start and end apart: 30, of which 19 were waited for; matrix products, arithmetic and copies ran while one was open for 8% of the time, Pallas kernels for 0%

commit v1 on v0

v1 whole, which is shorter than its diff:
```python
import functools

import jax
import jax.numpy as jnp
from jax import lax
from jax.experimental import pallas as pl
from jax.experimental.pallas import tpu as pltpu
from jax.sharding import PartitionSpec as P

MESH = pl.DeviceIdType.MESH
F32 = jnp.float32
BF16 = jnp.bfloat16
PAD = 4
ROWS = 8
LANES = 128


def iota(shape, dim):
    return lax.broadcasted_iota(jnp.int32, shape, dim)


def logical(index, own, extra):
    if extra == 0:
        return index
    return jnp.where(index < own + extra // 2, index, index - (own + extra))


def prolong_matrix(fine, coarse, total, fine_dim):
    base = lax.shift_right_arithmetic(fine, 1)
    beside = base + 2 * (fine & 1) - 1
    inside = jnp.logical_and(fine >= 0, fine < total)
    value = jnp.where(coarse == base, 0.75, jnp.where(coarse == beside, 0.25, 0.0))
    return jnp.where(inside, value, 0.0).astype(BF16)


def split(values):
    high = values.astype(BF16)
    return high, (values - high.astype(F32)).astype(BF16)


def mm(a, b):
    return jnp.dot(a, b, preferred_element_type=F32)


def fold_rows(values):
    total = values[0:ROWS]
    for row in range(ROWS, values.shape[0], ROWS):
        total = total + values[row : row + ROWS]
    out = total[:, 0:LANES]
    for lane in range(LANES, values.shape[1], LANES):
        out = out + total[:, lane : lane + LANES]
    return out


def coefficients(m0, n1, n2, n3):
    rho = n1 / m0
    spread = n2 - rho * n1
    bent = 6.0 * spread + (n3 - 2.0 * rho * n2 + rho * rho * n1)
    turn = jnp.where(bent > 0.0, jnp.maximum(spread, 0.0) / bent, 0.0)
    first = m0 / ((6.0 + rho) * m0 - jnp.maximum(spread, 0.0) * turn)
    second = -first * turn
    return first - second * rho, second


def kernel(
    dims,
    rhs_c, rhs_m, rhs_f, occ_c, occ_m, occ_f, weight,
    out_c, out_m, out_f,
    cr, cw, cs, cx, ctz, ct, oc,
    mb, mg, mr, mw, ms, mx, mtz, mt, om, m_up, m_dn, m_fu, m_fd, om_l, om_r,
    fb, fg, fr, fw, fs, of, f_up, f_dn, f_fu, f_fd, of_l, of_r,
    am, af, ss, rs, sm, rm, sf, rf,
):
    nx, ny, nz = dims
    ix, iy, iz = lax.axis_index("gx"), lax.axis_index("gy"), lax.axis_index("gz")
    xc, yc, zc = rhs_c.shape
    xm, ym, zm = rhs_m.shape
    xf, yf, zf = rhs_f.shape
    bc, bm, bf = occ_c.shape, occ_m.shape, occ_f.shape
    total_xc = xc * nx
    x_low, x_high = ix > 0, ix < nx - 1
    y_low, y_high = iy > 0, iy < ny - 1

    for ref in (om, of):
        ref[...] = jnp.zeros_like(ref)
    own_x = pl.ds(ix * xc + 3, xc)
    own_bx = pl.ds(ix * bc[0], bc[0])
    cr[own_x] = rhs_c[...].astype(F32)
    oc[own_bx] = jnp.zeros((bc[0],) + tuple(oc.shape[1:]), F32)
    oc[own_bx, 0 : bc[1], 0 : bc[2]] = occ_c[...].astype(F32)
    om[1 : 1 + bm[0], 0 : bm[1], 0 : bm[2]] = occ_m[...].astype(F32)
    of[1 : 1 + bf[0], 0 : bf[1], 0 : bf[2]] = occ_f[...].astype(F32)
    mb[PAD : PAD + xm, 0:ym, :] = rhs_m[...].astype(F32)

    def fill_fine(x, carry):
        fb[x + PAD, 0:yf, 0:zf] = rhs_f[x].astype(F32)
        return carry

    lax.fori_loop(0, xf, fill_fine, 0)

    barrier = pltpu.get_barrier_semaphore()
    peers = [(a, b, c) for a in range(nx) for b in range(ny) for c in range(nz)][1:]

    def at(offset):
        return (
            lax.rem(ix + offset[0], nx), lax.rem(iy + offset[1], ny), lax.rem(iz + offset[2], nz)
        )

    for offset in peers:
        pl.semaphore_signal(barrier, inc=1, device_id=at(offset), device_id_type=MESH)

    zero_c = jnp.zeros((3, yc, zc), F32)
    cr[0:3] = zero_c
    cr[total_xc + 3 : total_xc + 6] = zero_c
    cw[0:3] = zero_c
    cw[total_xc + 3 : total_xc + 6] = zero_c

    @pl.when(jnp.logical_not(x_low))
    def _():
        mb[1:4, 0:ym, :] = jnp.zeros((3, ym, zm), F32)
        fb[2:4, 0:yf, :] = jnp.zeros((2, yf, fb.shape[2]), F32)

    @pl.when(jnp.logical_not(x_high))
    def _():
        mb[PAD + xm : PAD + xm + 3, 0:ym, :] = jnp.zeros((3, ym, zm), F32)
        fb[PAD + xf : PAD + xf + 2, 0:yf, :] = jnp.zeros((2, yf, fb.shape[2]), F32)

    @pl.when(jnp.logical_not(y_low))
    def _():
        for ref in (m_fu, f_fu, om_l, of_l):
            ref[...] = jnp.zeros_like(ref)

    @pl.when(jnp.logical_not(y_high))
    def _():
        for ref in (m_fd, f_fd, om_r, of_r):
            ref[...] = jnp.zeros_like(ref)

    pl.semaphore_wait(barrier, len(peers))

    used = [0]

    def copy(src, dst, target):
        k = used[0]
        used[0] += 1
        return pltpu.make_async_remote_copy(
            src_ref=src, dst_ref=dst, send_sem=ss.at[k], recv_sem=rs.at[k],
            device_id=target, device_id_type=MESH,
        )

    sends = []

    def start(items):
        for c, can_send, _ in items:
            if can_send is None:
                c.start()
            else:
                pl.when(can_send)(c.start)
        sends.extend(items)

    def arrive(items):
        for c, _, can_recv in items:
            if can_recv is None:
                c.wait_recv()
            else:
                pl.when(can_recv)(c.wait_recv)

    def left(items):
        for c, can_send, _ in items:
            if can_send is None:
                c.wait_send()
            else:
                pl.when(can_send)(c.wait_send)

    gather = []
    for d in range(1, nx):
        target = {"gx": lax.rem(ix + d, nx)}
        gather.append((d, copy(cr.at[own_x], cr.at[own_x], target), None))
        gather.append((d, copy(oc.at[own_bx], oc.at[own_bx], target), None))
    for _, c, _ in gather:
        c.start()
    z_fine = []
    if nz == 2:
        target = {"gz": 1 - iz}
        low = pl.ds(pl.multiple_of((1 - iz) * (zf - LANES), LANES), LANES)
        z_fine.append((copy(
            fb.at[PAD : PAD + xf, 0:yf, low],
            fb.at[PAD : PAD + xf, 0:yf, zf : zf + LANES], target), None, None))
        z_fine.append((copy(
            of.at[1 : 1 + bf[0], :, 0:LANES], of.at[1 : 1 + bf[0], :, LANES : 2 * LANES],
            target), None, None))
    else:
        fb[PAD : PAD + xf, 0:yf, zf:] = jnp.zeros((xf, yf, LANES), F32)
    start(z_fine)

    def x_swap(ref, occ, own, rows, width, bricks):
        items = []
        up, down = {"gx": ix + 1}, {"gx": ix - 1}
        items.append((copy(ref.at[PAD + own - width : PAD + own, 0:rows, :],
                           ref.at[PAD - width : PAD, 0:rows, :], up), x_high, x_low))
        items.append((copy(ref.at[PAD : PAD + width, 0:rows, :],
                           ref.at[PAD + own : PAD + own + width, 0:rows, :], down), x_low, x_high))
        items.append((copy(occ.at[bricks], occ.at[0], up), x_high, x_low))
        items.append((copy(occ.at[1], occ.at[bricks + 1], down), x_low, x_high))
        return items

    def y_swap(ref, occ, own, width, to_up, to_down, from_low, from_high, occ_l, occ_r, planes):
        first, count = planes
        to_up[...] = ref[first : first + count, own - width : own, :]
        to_down[...] = ref[first : first + count, 0:width, :]
        up, down = {"gy": iy + 1}, {"gy": iy - 1}
        return [
            (copy(to_up, from_low, up), y_high, y_low),
            (copy(to_down, from_high, down), y_low, y_high),
            (copy(occ, occ_l, up), y_high, y_low),
            (copy(occ, occ_r, down), y_low, y_high),
        ]

    def y_merge(ref, own, width, from_low, from_high, planes):
        first, count = planes
        parts = [from_high[...], from_low[...]]
        if 2 * width < ROWS:
            parts.insert(1, jnp.zeros((count, ROWS - 2 * width, ref.shape[2]), F32))
        ref[first : first + count, own : own + ROWS, :] = jnp.concatenate(parts, axis=1)

    x_mid = x_swap(mb, om, xm, ym, 3, bm[0])
    start(x_mid)
    mid_planes, fine_planes = (1, xm + 6), (2, xf + 4)

    def row_prolong(own, extra, index, total, cols, col_own, col_extra, col_index):
        shape = (own + extra, cols)
        fine = logical(iota(shape, 0), own, extra) + own * index
        coarse = logical(iota(shape, 1), col_own, col_extra) + col_own * col_index
        return prolong_matrix(fine, coarse, total, 0)

    def lane_prolong(own, extra, index, total, rows):
        shape = (rows, own + extra)
        fine = logical(iota(shape, 1), own, extra) + own * index
        return prolong_matrix(fine, iota(shape, 0), total, 1)

    def screens(dest, occ_parts, own, extra_rows, bricks_y, lane_matrix, level):
        count = dest.shape[0]
        side = own // bricks_y
        cols = ROWS * len(occ_parts)
        shape = (dest.shape[1], cols)
        brick = lax.div(logical(iota(shape, 0), own, extra_rows) + side, side) - 1
        place = jnp.where(
            brick < 0, ROWS + bricks_y - 1, jnp.where(brick >= bricks_y, 2 * ROWS, brick)
        )
        row_matrix = (place == iota(shape, 1)).astype(BF16)
        for x in range(count):
            flags = jnp.concatenate([part[x] for part in occ_parts], axis=0).astype(BF16)
            wide = mm(flags, lane_matrix).astype(BF16)
            dest[x] = weight[level] * (0.25 + mm(row_matrix, wide))

    def along_y(v):
        n = v.shape[0]
        return pltpu.roll(v, 1, 0), pltpu.roll(v, n - 1, 0)

    def along_z(v):
        n = v.shape[1]
        return pltpu.roll(v, 1, 1), pltpu.roll(v, n - 1, 1)

    arrive(z_fine)
    x_fine = x_swap(fb, of, xf, yf, 2, bf[0])
    start(x_fine)
    arrive(x_mid)
    y_mid = y_swap(mb, om, ym, 4, m_up, m_dn, m_fu, m_fd, om_l, om_r, mid_planes)
    start(y_mid)
    for _, c, _ in gather:
        c.wait_recv()

    lanes_c = (iota((LANES, zc), 0) == lax.div(iota((LANES, zc), 1), zc // bc[2])).astype(BF16)
    screens(cs, [oc], yc, 0, bc[1], lanes_c, 0)
    side_c = xc // bc[0]
    shape_c = (yc, zc)
    row_c, lane_c = iota(shape_c, 0), iota(shape_c, 1)

    def sum_c(v, both):
        yu, yd = along_y(v)
        zu, zd = along_z(v)
        total = jnp.where(row_c < yc - 1, yd, 0.0) + jnp.where(lane_c < zc - 1, zd, 0.0)
        if both:
            total = total + jnp.where(row_c > 0, yu, 0.0) + jnp.where(lane_c > 0, zu, 0.0)
        return total

    def coarse_w(x, carry):
        r = cr[x + 3]
        cw[x + 3] = cs[lax.div(x, side_c)] * r - (cr[x + 2] + cr[x + 4] + sum_c(r, True))
        return carry

    lax.fori_loop(0, total_xc, coarse_w, 0)

    arrive(x_fine)
    y_fine = y_swap(fb, of, yf, 2, f_up, f_dn, f_fu, f_fd, of_l, of_r, fine_planes)
    start(y_fine)

    def coarse_moments(x, acc):
        r, w = cr[x + 3], cw[x + 3]
        image = cs[lax.div(x, side_c)] * w - 2.0 * (cw[x + 4] + sum_c(w, False))
        return tuple(a + fold_rows(b) for a, b in zip(acc, (r * r, r * w, w * w, w * image)))

    zero = jnp.zeros((ROWS, LANES), F32)

    def whole_sum(v):
        return jnp.sum(jnp.sum(v, axis=0, keepdims=True), axis=1, keepdims=True)

    acc = lax.fori_loop(0, total_xc, coarse_moments, (zero,) * 4)
    ka, kb = coefficients(*[whole_sum(a) for a in acc])
    for j in range(xc + 6):
        cx[j] = ka * cr[ix * xc + j] + kb * cw[ix * xc + j]
    out_c[...] = cx[3 : 3 + xc]

    def prolong(src, tz, dst, lane_matrix, row_matrix):
        n, rows, lanes = src.shape
        high, low = split(src[...].reshape(n * rows, lanes))
        tz[...] = (mm(high, lane_matrix) + mm(low, lane_matrix)).reshape(tz.shape)
        for j in range(n):
            high, low = split(tz[j])
            dst[j] = mm(row_matrix, high) + mm(row_matrix, low)

    def interpolate(t, g, own, first, total):
        for p in range(own + 2 * PAD):
            m = p - PAD
            j = m // 2
            beside = min(max(j + (1 if m % 2 else -1) - first, 0), t.shape[0] - 1)
            place = own * ix + m
            keep = jnp.logical_and(place >= 0, place < total).astype(F32)
            g[p] = (0.75 * keep) * t[j - first] + (0.25 * keep) * t[beside]

    def neighbours(v, low_lane, high_lane):
        yu, yd = along_y(v)
        zu, zd = along_z(v)
        if low_lane is not None:
            zu, zd = jnp.where(low_lane, 0.0, zu), jnp.where(high_lane, 0.0, zd)
        return yu + yd + zu + zd

    def later(v, high_lane):
        yd = along_y(v)[1]
        zd = along_z(v)[1]
        if high_lane is not None:
            zd = jnp.where(high_lane, 0.0, zd)
        return yd + zd

    def run_depth(b, g, r, w, s, own, rows, lanes, reach, side, ends, mask):
        low_lane, high_lane = ends
        total_x = own * nx

        def inside(p):
            place = own * ix + p - PAD
            return jnp.logical_and(place >= 0, place < total_x).astype(F32)

        def brick(p):
            return lax.div(p + (side - PAD), side)

        def make_r(p, carry):
            c = g[p]
            value = b[p] - (6.0 + s[brick(p)]) * c
            value = value + (g[p - 1] + g[p + 1]) + neighbours(c, low_lane, high_lane)
            r[p] = value * (mask * inside(p))
            return carry

        lax.fori_loop(PAD - reach, PAD + own + reach, make_r, 0)

        def make_w(p, carry):
            c = r[p]
            value = s[brick(p)] * c - (r[p - 1] + r[p + 1]) - neighbours(c, low_lane, high_lane)
            w[p] = value * (mask * inside(p))
            return carry

        lax.fori_loop(PAD - reach + 1, PAD + own + reach - 1, make_w, 0)

        def moments(p, acc):
            rv, wv = r[p, 0:rows, 0:lanes], w[p, 0:rows, 0:lanes]
            full = w[p]
            image = s[brick(p), 0:rows, 0:lanes] * wv - 2.0 * (
                w[p + 1, 0:rows, 0:lanes] + later(full, high_lane)[0:rows, 0:lanes]
            )
            return tuple(
                a + fold_rows(v) for a, v in zip(acc, (rv * rv, rv * wv, wv * wv, wv * image))
            )

        return lax.fori_loop(PAD, PAD + own, moments, (zero,) * 4)

    def exchange(acc, buf, send, recv, offsets, slot):
        parts = [jnp.sum(a, axis=0, keepdims=True) for a in acc]
        buf[slot] = jnp.concatenate(parts + [jnp.zeros((ROWS - 4, LANES), F32)], axis=0)
        copies = []
        for k, offset in enumerate(offsets):
            c = pltpu.make_async_remote_copy(
                src_ref=buf.at[slot], dst_ref=buf.at[slot], send_sem=send.at[k],
                recv_sem=recv.at[k], device_id=at(offset), device_id_type=MESH,
            )
            c.start()
            copies.append(c)
        for c in copies:
            c.wait_recv()
        total = buf[0]
        for k in range(1, buf.shape[0]):
            total = total + buf[k]
        total = jnp.sum(total, axis=1, keepdims=True)
        return coefficients(*[total[k : k + 1] for k in range(4)]), copies

    prolong(
        cx, ctz, ct, lane_prolong(zm, 0, 0, zm, zc),
        row_prolong(ym, ROWS, iy, ym * ny, yc, yc, 0, 0),
    )
    interpolate(ct, mg, xm, -3, xm * nx)
    arrive(y_mid)
    left(x_mid)
    y_merge(mb, ym, 4, m_fu, m_fd, mid_planes)
    lanes_m = (iota((LANES, zm), 0) == lax.div(iota((LANES, zm), 1), zm // bm[2])).astype(BF16)
    screens(ms, [om, om_l, om_r], ym, ROWS, bm[1], lanes_m, 1)
    shape_m = (ym + ROWS, zm)
    row_m = logical(iota(shape_m, 0), ym, ROWS) + ym * iy
    mask_m = jnp.logical_and(row_m >= 0, row_m < ym * ny).astype(F32)
    ends_m = (iota(shape_m, 1) == 0, iota(shape_m, 1) == zm - 1)
    acc = run_depth(mb, mg, mr, mw, ms, xm, ym, zm, 3, xm // bm[0], ends_m, mask_m)
    flat = [o for o in peers if o[2] == 0]
    (ka, kb), mid_copies = exchange(acc, am, sm, rm, flat, ix * ny + iy)
    for p in range(2, xm + 6):
        value = mg[p] + ka * mr[p] + kb * mw[p]
        mx[p - 2] = value
        if PAD <= p < PAD + xm:
            out_m[p - PAD] = value[0:ym]

    prolong(
        mx, mtz, mt, lane_prolong(zf, LANES, iz, zf * nz, zm),
        row_prolong(yf, ROWS, iy, yf * ny, ym + ROWS, ym, ROWS, iy),
    )
    interpolate(mt, fg, xf, -2, xf * nx)
    arrive(y_fine)
    left(x_fine)
    left(z_fine)
    y_merge(fb, yf, 2, f_fu, f_fd, fine_planes)
    shape_e = (2 * LANES, zf + LANES)
    cell = logical(iota(shape_e, 1), zf, LANES)
    side_z = zf // bf[2]
    brick = lax.div(cell + side_z * LANES, side_z) - LANES
    place = jnp.where(
        brick < 0, LANES + bf[2] + brick, jnp.where(brick >= bf[2], LANES + brick - bf[2], brick)
    )
    lanes_f = (place == iota(shape_e, 0)).astype(BF16)
    screens(fs, [of, of_l, of_r], yf, ROWS, bf[1], lanes_f, 2)
    shape_f = (yf + ROWS, zf + LANES)
    row_f = logical(iota(shape_f, 0), yf, ROWS) + yf * iy
    lane_f = logical(iota(shape_f, 1), zf, LANES) + zf * iz
    mask_f = jnp.logical_and(
        jnp.logical_and(row_f >= 0, row_f < yf * ny), jnp.logical_and(lane_f >= 0, lane_f < zf * nz)
    ).astype(F32)
    acc = run_depth(fb, fg, fr, fw, fs, xf, yf, zf, 2, xf // bf[0], (None, None), mask_f)
    (ka, kb), fine_copies = exchange(acc, af, sf, rf, peers, (ix * ny + iy) * nz + iz)

    def finish(x, carry):
        p = x + PAD
        out_f[x] = (
            fg[p, 0:yf, 0:zf] + ka * fr[p, 0:yf, 0:zf] + kb * fw[p, 0:yf, 0:zf]
        )
        return carry

    lax.fori_loop(0, xf, finish, 0)

    for _, c, _ in gather:
        c.wait_send()
    left(not_in(sends, x_mid + x_fine + z_fine))
    for c in mid_copies + fine_copies:
        c.wait_send()


def not_in(items, waited):
    done = [id(item) for item in waited]
    return [item for item in items if id(item) not in done]


def shards(dims, *args):
    nx, ny, nz = dims
    rhs_c, rhs_m, rhs_f, occ_c, occ_m, occ_f, _ = args
    xc, yc, zc = rhs_c.shape
    xm, ym, zm = rhs_m.shape
    xf, yf, zf = rhs_f.shape
    me, fe = (ym + ROWS, zm), (yf + ROWS, zf + LANES)

    def buf(*shape):
        return pltpu.VMEM(shape, F32)

    bm, bf = occ_m.shape[0] + 2, occ_f.shape[0] + 2
    scratch = [
        buf(xc * nx + 6, yc, zc), buf(xc * nx + 6, yc, zc), buf(occ_c.shape[0] * nx, yc, zc),
        buf(xc + 6, yc, zc), buf(xc + 6, yc, zm), buf(xc + 6, *me),
        buf(occ_c.shape[0] * nx, ROWS, LANES),
        buf(xm + 8, *me), buf(xm + 8, *me), buf(xm + 8, *me), buf(xm + 8, *me), buf(bm, *me),
        buf(xm + 4, *me), buf(xm + 4, me[0], fe[1]), buf(xm + 4, *fe),
        buf(bm, ROWS, LANES),
        buf(xm + 6, 4, zm), buf(xm + 6, 4, zm), buf(xm + 6, 4, zm), buf(xm + 6, 4, zm),
        buf(bm, ROWS, LANES), buf(bm, ROWS, LANES),
        buf(xf + 8, *fe), buf(xf + 8, *fe), buf(xf + 8, *fe), buf(xf + 8, *fe), buf(bf, *fe),
        buf(bf, ROWS, 2 * LANES),
        buf(xf + 4, 2, fe[1]), buf(xf + 4, 2, fe[1]), buf(xf + 4, 2, fe[1]), buf(xf + 4, 2, fe[1]),
        buf(bf, ROWS, 2 * LANES), buf(bf, ROWS, 2 * LANES),
        buf(nx * ny, ROWS, LANES), buf(nx * ny * nz, ROWS, LANES),
        pltpu.SemaphoreType.DMA((2 * nx + 16,)), pltpu.SemaphoreType.DMA((2 * nx + 16,)),
        pltpu.SemaphoreType.DMA((nx * ny,)), pltpu.SemaphoreType.DMA((nx * ny,)),
        pltpu.SemaphoreType.DMA((nx * ny * nz,)), pltpu.SemaphoreType.DMA((nx * ny * nz,)),
    ]
    vmem = pl.BlockSpec(memory_space=pltpu.VMEM)
    return pl.pallas_call(
        functools.partial(kernel, dims),
        out_shape=[jax.ShapeDtypeStruct(a.shape, F32) for a in args[:3]],
        in_specs=[vmem] * 6 + [pl.BlockSpec(memory_space=pltpu.SMEM)],
        out_specs=[vmem] * 3,
        scratch_shapes=scratch,
        compiler_params=pltpu.CompilerParams(
            collective_id=0, has_side_effects=True, vmem_limit_bytes=60 * 1024 * 1024
        ),
    )(*args)


def solution(mesh):
    dims = tuple(mesh.shape[axis] for axis in ("gx", "gy", "gz"))
    in_specs = (
        P("gx", None, None), P("gx", "gy", None), P("gx", "gy", "gz"),
        P("gx", None, None), P("gx", "gy", None), P("gx", "gy", "gz"), P(),
    )
    out_specs = (P("gx", None, None), P("gx", "gy", None), P("gx", "gy", "gz"))
    return jax.shard_map(
        functools.partial(shards, dims), mesh=mesh, in_specs=in_specs, out_specs=out_specs,
        check_vma=False,
    )
```

time: 497 us -> 63.7 us (0.13)
  blocking collectives: 265 us -> 0 us
  starting transfers between devices: 69.6 us -> 0 us
  Pallas kernels: 0 us -> 58.2 us
  local copies, waits for them, and re-layouts: 58.1 us -> 4.62 us
  waiting for transfers between devices: 48.5 us -> 0 us
  other arithmetic: 40.6 us -> 0 us
  between operations: 13.6 us -> 0.65 us
    psum x9 -> x0, blocking collectives: 265 us -> none  [the longest x3 119 us: level_sum(): return lax.psum((values[0],), ('gx', 'gy', 'gz'))]
    ppermute x30 -> x0, starting transfers between devices: 69.6 us -> none  [the longest x15 50.1 us: extended_2(): before = lax.ppermute(last, axis, up)]
    pallas_call x0 -> x1, Pallas kernels: none -> 58.2 us  [shards(): pl.pallas_call(functools.partial(kernel, dims), out_shape=[jax.ShapeDtype...]
    ppermute x30 -> x0, waiting for transfers between devices: 48.5 us -> none  [the longest x15 46.7 us: extended_2(): after = lax.ppermute(first, axis, down)]
    reduce_sum x9 -> x0, other arithmetic: 20.9 us -> none  [the longest x6 17.4 us: cg_solve(): curvature, = level_sum((jnp.sum(direction * image),), depth_level)]
    add x7 -> x0, local copies, waits for them, and re-layouts: 17.8 us -> none  [the longest x3 17.7 us: stencil(): return (6.0 + screen) * centre - beside]
    broadcast_in_dim x3 -> x0, local copies, waits for them, and re-layouts: 10.6 us -> none  [screening(): jnp.broadcast_to(brick_flags[:, None, :, None, :, None], (brick_shape[0],...]
    add x15 -> x0, other arithmetic: 9.77 us -> none  [the longest x3 3.32 us: stencil(): return (6.0 + screen) * centre - beside]
  transfers between devices with their start and end apart: 30 -> 0, of which waited for: 19 -> 0; matrix products, arithmetic and copies ran while one was open for 8% -> 0% of each run, Pallas kernels for 0% -> 0%
where the time goes in v1:
time: 63.7 us; the launch traced here: 63.5 us
  Pallas kernels  58.2 us (91%)
  local copies, waits for them, and re-layouts  4.62 us (7%)
  between operations  0.65 us (1%)
    pallas_call x1, Pallas kernels, shards(): pl.pallas_call(functools.partial(kernel, dims), out_shape=[jax.ShapeDtype...  58.2 us
    unnamed x5, local copies, waits for them, and re-layouts  4.62 us

profile of v1, /device:TPU:0, one launch (start us, length us, event | category | flops | bytes accessed | tf_op | source)
XLA Modules:
  0.0 63.5 jit_solution(5022724293762735293)
XLA Ops:
  0.6 58.2 %shard_map.94 = (f32[8,32,128]{2,1,0:T(8,128)}, f32[16,16,256]{2,1,0:T(8,128)}, f32[32,32,256]{2,1,0:T(8,128)}) custom-call(bf16[8,32,128]{2,1,0:T(8,128)(2,1)} %rhs_c.1, bf16[16,16,256]{2,1,0:T(8,128)(2,1)} %rhs_m.1, bf16[32,32,256]{2,1,0:T(8,128)(2,1)} %rhs_f.1, s32[1,4,16]{2,1,0:T(4,128)} %occ_c.1, s32[2,2,32]{2,1,0:T(2,128)} %occ_m.1, ...), custom_call_target="tpu_custom_call" | custom-call | tf_op jit(solution)/shard_map/pallas_call | solution.py:505
  58.8 0.0 copy-start
  58.8 1.6 %copy.13 = f32[8,32,128]{2,1,0:T(8,128)} copy(f32[8,32,128]{2,1,0:T(8,128)} %get-tuple-element.6) | data formatting | bytes 262144
  60.4 0.0 copy-done
  60.5 0.7 %copy.14 = f32[16,16,256]{2,1,0:T(8,128)} copy(f32[16,16,256]{2,1,0:T(8,128)S(1)} %copy-done) | data formatting | bytes 524288
  61.2 2.3 %copy.15 = f32[32,32,256]{2,1,0:T(8,128)} copy(f32[32,32,256]{2,1,0:T(8,128)} %get-tuple-element.8) | data formatting | bytes 2097152
Async XLA Ops:
  58.8 1.6 %copy-start = (f32[16,16,256]{2,1,0:T(8,128)S(1)}, f32[16,16,256]{2,1,0:T(8,128)}, u32[]{:S(2)}) copy-start(f32[16,16,256]{2,1,0:T(8,128)} %get-tuple-element.7) | copy-start | bytes 786436

commit v2 on v1

--- a/solution.py
+++ b/solution.py
@@ -69,7 +69,7 @@
     cr, cw, cs, cx, ctz, ct, oc,
     mb, mg, mr, mw, ms, mx, mtz, mt, om, m_up, m_dn, m_fu, m_fd, om_l, om_r,
     fb, fg, fr, fw, fs, of, f_up, f_dn, f_fu, f_fd, of_l, of_r,
-    am, af, ss, rs, sm, rm, sf, rf,
+    ac, am, af, ag, ss, rs, sc, rc, sm, rm, sf, rf, sg, rg,
 ):
     nx, ny, nz = dims
     ix, iy, iz = lax.axis_index("gx"), lax.axis_index("gy"), lax.axis_index("gz")
@@ -77,17 +77,13 @@
     xm, ym, zm = rhs_m.shape
     xf, yf, zf = rhs_f.shape
     bc, bm, bf = occ_c.shape, occ_m.shape, occ_f.shape
-    total_xc = xc * nx
     x_low, x_high = ix > 0, ix < nx - 1
     y_low, y_high = iy > 0, iy < ny - 1
 
-    for ref in (om, of):
+    for ref in (oc, om, of):
         ref[...] = jnp.zeros_like(ref)
-    own_x = pl.ds(ix * xc + 3, xc)
-    own_bx = pl.ds(ix * bc[0], bc[0])
-    cr[own_x] = rhs_c[...].astype(F32)
-    oc[own_bx] = jnp.zeros((bc[0],) + tuple(oc.shape[1:]), F32)
-    oc[own_bx, 0 : bc[1], 0 : bc[2]] = occ_c[...].astype(F32)
+    cr[PAD : PAD + xc] = rhs_c[...].astype(F32)
+    oc[1 : 1 + bc[0], 0 : bc[1], 0 : bc[2]] = occ_c[...].astype(F32)
     om[1 : 1 + bm[0], 0 : bm[1], 0 : bm[2]] = occ_m[...].astype(F32)
     of[1 : 1 + bf[0], 0 : bf[1], 0 : bf[2]] = occ_f[...].astype(F32)
     mb[PAD : PAD + xm, 0:ym, :] = rhs_m[...].astype(F32)
@@ -99,7 +95,9 @@
     lax.fori_loop(0, xf, fill_fine, 0)
 
     barrier = pltpu.get_barrier_semaphore()
-    peers = [(a, b, c) for a in range(nx) for b in range(ny) for c in range(nz)][1:]
+    flat = [(a, b, 0) for a in range(nx) for b in range(ny)][1:]
+    across = [(0, 0, c) for c in range(1, nz)]
+    peers = flat + across
 
     def at(offset):
         return (
@@ -109,21 +107,33 @@
     for offset in peers:
         pl.semaphore_signal(barrier, inc=1, device_id=at(offset), device_id_type=MESH)
 
-    zero_c = jnp.zeros((3, yc, zc), F32)
-    cr[0:3] = zero_c
-    cr[total_xc + 3 : total_xc + 6] = zero_c
-    cw[0:3] = zero_c
-    cw[total_xc + 3 : total_xc + 6] = zero_c
-
     @pl.when(jnp.logical_not(x_low))
     def _():
+        cr[0:4] = jnp.zeros((4, yc, zc), F32)
         mb[1:4, 0:ym, :] = jnp.zeros((3, ym, zm), F32)
         fb[2:4, 0:yf, :] = jnp.zeros((2, yf, fb.shape[2]), F32)
 
     @pl.when(jnp.logical_not(x_high))
     def _():
+        cr[PAD + xc : PAD + xc + 4] = jnp.zeros((4, yc, zc), F32)
         mb[PAD + xm : PAD + xm + 3, 0:ym, :] = jnp.zeros((3, ym, zm), F32)
         fb[PAD + xf : PAD + xf + 2, 0:yf, :] = jnp.zeros((2, yf, fb.shape[2]), F32)
+
+    @pl.when(jnp.logical_not(x_low))
+    def _():
+        for ref, reach in ((m_fu, 3), (m_fd, 3), (f_fu, 2), (f_fd, 2)):
+            ref[0:reach] = jnp.zeros((reach,) + tuple(ref.shape[1:]), F32)
+        for ref in (om_l, om_r, of_l, of_r):
+            ref[0:1] = jnp.zeros((1,) + tuple(ref.shape[1:]), F32)
+
+    @pl.when(jnp.logical_not(x_high))
+    def _():
+        for ref, reach in ((m_fu, 3), (m_fd, 3), (f_fu, 2), (f_fd, 2)):
+            size = ref.shape[0]
+            ref[size - reach : size] = jnp.zeros((reach,) + tuple(ref.shape[1:]), F32)
+        for ref in (om_l, om_r, of_l, of_r):
+            size = ref.shape[0]
+            ref[size - 1 : size] = jnp.zeros((1,) + tuple(ref.shape[1:]), F32)
 
     @pl.when(jnp.logical_not(y_low))
     def _():
@@ -147,15 +157,12 @@
             device_id=target, device_id_type=MESH,
         )
 
-    sends = []
-
     def start(items):
         for c, can_send, _ in items:
             if can_send is None:
                 c.start()
             else:
                 pl.when(can_send)(c.start)
-        sends.extend(items)
 
     def arrive(items):
         for c, _, can_recv in items:
@@ -170,27 +177,6 @@
                 c.wait_send()
             else:
                 pl.when(can_send)(c.wait_send)
-
-    gather = []
-    for d in range(1, nx):
-        target = {"gx": lax.rem(ix + d, nx)}
-        gather.append((d, copy(cr.at[own_x], cr.at[own_x], target), None))
-        gather.append((d, copy(oc.at[own_bx], oc.at[own_bx], target), None))
-    for _, c, _ in gather:
-        c.start()
-    z_fine = []
-    if nz == 2:
-        target = {"gz": 1 - iz}
-        low = pl.ds(pl.multiple_of((1 - iz) * (zf - LANES), LANES), LANES)
-        z_fine.append((copy(
-            fb.at[PAD : PAD + xf, 0:yf, low],
-            fb.at[PAD : PAD + xf, 0:yf, zf : zf + LANES], target), None, None))
-        z_fine.append((copy(
-            of.at[1 : 1 + bf[0], :, 0:LANES], of.at[1 : 1 + bf[0], :, LANES : 2 * LANES],
-            target), None, None))
-    else:
-        fb[PAD : PAD + xf, 0:yf, zf:] = jnp.zeros((xf, yf, LANES), F32)
-    start(z_fine)
 
     def x_swap(ref, occ, own, rows, width, bricks):
         items = []
@@ -203,17 +189,31 @@
         items.append((copy(occ.at[1], occ.at[bricks + 1], down), x_low, x_high))
         return items
 
-    def y_swap(ref, occ, own, width, to_up, to_down, from_low, from_high, occ_l, occ_r, planes):
-        first, count = planes
-        to_up[...] = ref[first : first + count, own - width : own, :]
-        to_down[...] = ref[first : first + count, 0:width, :]
-        up, down = {"gy": iy + 1}, {"gy": iy - 1}
-        return [
-            (copy(to_up, from_low, up), y_high, y_low),
-            (copy(to_down, from_high, down), y_low, y_high),
-            (copy(occ, occ_l, up), y_high, y_low),
-            (copy(occ, occ_r, down), y_low, y_high),
-        ]
+    x_coarse = x_swap(cr, oc, xc, yc, 4, bc[0])
+    start(x_coarse)
+
+    def y_swap(ref, occ, own, rows, width, reach, to_up, to_down, from_low, from_high, occ_l, occ_r, bricks):
+        planes, flags = pl.ds(reach, own), pl.ds(1, bricks)
+        to_up[planes] = ref[PAD : PAD + own, rows - width : rows, :]
+        to_down[planes] = ref[PAD : PAD + own, 0:width, :]
+        items = []
+        for out, dst, occ_dst, step, can_send, can_recv in (
+            (to_up, from_low, occ_l, 1, y_high, y_low), (to_down, from_high, occ_r, -1, y_low, y_high)
+        ):
+            side = {"gy": iy + step}
+            items.append((copy(out.at[planes], dst.at[planes], side), can_send, can_recv))
+            items.append((copy(occ.at[flags], occ_dst.at[flags], side), can_send, can_recv))
+            corner = {"gx": ix + 1, "gy": iy + step}
+            when = (jnp.logical_and(can_send, x_high), jnp.logical_and(can_recv, x_low))
+            items.append((copy(out.at[pl.ds(own, reach)], dst.at[pl.ds(0, reach)], corner), *when))
+            items.append((copy(occ.at[bricks], occ_dst.at[0], corner), *when))
+            corner = {"gx": ix - 1, "gy": iy + step}
+            when = (jnp.logical_and(can_send, x_low), jnp.logical_and(can_recv, x_high))
+            items.append(
+                (copy(out.at[pl.ds(reach, reach)], dst.at[pl.ds(own + reach, reach)], corner), *when)
+            )
+            items.append((copy(occ.at[1], occ_dst.at[bricks + 1], corner), *when))
+        return items
 
     def y_merge(ref, own, width, from_low, from_high, planes):
         first, count = planes
@@ -222,8 +222,6 @@
             parts.insert(1, jnp.zeros((count, ROWS - 2 * width, ref.shape[2]), F32))
         ref[first : first + count, own : own + ROWS, :] = jnp.concatenate(parts, axis=1)
 
-    x_mid = x_swap(mb, om, xm, ym, 3, bm[0])
-    start(x_mid)
     mid_planes, fine_planes = (1, xm + 6), (2, xf + 4)
 
     def row_prolong(own, extra, index, total, cols, col_own, col_extra, col_index):
@@ -260,16 +258,24 @@
         n = v.shape[1]
         return pltpu.roll(v, 1, 1), pltpu.roll(v, n - 1, 1)
 
-    arrive(z_fine)
-    x_fine = x_swap(fb, of, xf, yf, 2, bf[0])
-    start(x_fine)
-    arrive(x_mid)
-    y_mid = y_swap(mb, om, ym, 4, m_up, m_dn, m_fu, m_fd, om_l, om_r, mid_planes)
-    start(y_mid)
-    for _, c, _ in gather:
-        c.wait_recv()
-
     lanes_c = (iota((LANES, zc), 0) == lax.div(iota((LANES, zc), 1), zc // bc[2])).astype(BF16)
+    arrive(x_coarse)
+    halo_mid = x_swap(mb, om, xm, ym, 3, bm[0])
+    halo_mid += y_swap(mb, om, xm, ym, 4, 3, m_up, m_dn, m_fu, m_fd, om_l, om_r, bm[0])
+    start(halo_mid)
+    z_fine = []
+    if nz == 2:
+        target = {"gz": 1 - iz}
+        low = pl.ds(pl.multiple_of((1 - iz) * (zf - LANES), LANES), LANES)
+        z_fine.append((copy(
+            fb.at[PAD : PAD + xf, 0:yf, low],
+            fb.at[PAD : PAD + xf, 0:yf, zf : zf + LANES], target), None, None))
+        z_fine.append((copy(
+            of.at[1 : 1 + bf[0], :, 0:LANES], of.at[1 : 1 + bf[0], :, LANES : 2 * LANES],
+            target), None, None))
+    else:
+        fb[PAD : PAD + xf, 0:yf, zf:] = jnp.zeros((xf, yf, LANES), F32)
+    start(z_fine)
     screens(cs, [oc], yc, 0, bc[1], lanes_c, 0)
     side_c = xc // bc[0]
     shape_c = (yc, zc)
@@ -283,31 +289,66 @@
             total = total + jnp.where(row_c > 0, yu, 0.0) + jnp.where(lane_c > 0, zu, 0.0)
         return total
 
-    def coarse_w(x, carry):
-        r = cr[x + 3]
-        cw[x + 3] = cs[lax.div(x, side_c)] * r - (cr[x + 2] + cr[x + 4] + sum_c(r, True))
+    def coarse_w(p, carry):
+        r = cr[p]
+        place = xc * ix + p - PAD
+        keep = jnp.logical_and(place >= 0, place < xc * nx).astype(F32)
+        screen = cs[lax.div(p + (side_c - PAD), side_c)]
+        cw[p] = keep * (screen * r - (cr[p - 1] + cr[p + 1] + sum_c(r, True)))
         return carry
 
-    lax.fori_loop(0, total_xc, coarse_w, 0)
-
-    arrive(x_fine)
-    y_fine = y_swap(fb, of, yf, 2, f_up, f_dn, f_fu, f_fd, of_l, of_r, fine_planes)
-    start(y_fine)
-
-    def coarse_moments(x, acc):
-        r, w = cr[x + 3], cw[x + 3]
-        image = cs[lax.div(x, side_c)] * w - 2.0 * (cw[x + 4] + sum_c(w, False))
+    lax.fori_loop(1, xc + 7, coarse_w, 0, unroll=2)
+
+    def coarse_moments(p, acc):
+        r, w = cr[p], cw[p]
+        screen = cs[lax.div(p + (side_c - PAD), side_c)]
+        image = screen * w - 2.0 * (cw[p + 1] + sum_c(w, False))
         return tuple(a + fold_rows(b) for a, b in zip(acc, (r * r, r * w, w * w, w * image)))
 
     zero = jnp.zeros((ROWS, LANES), F32)
 
-    def whole_sum(v):
-        return jnp.sum(jnp.sum(v, axis=0, keepdims=True), axis=1, keepdims=True)
-
-    acc = lax.fori_loop(0, total_xc, coarse_moments, (zero,) * 4)
-    ka, kb = coefficients(*[whole_sum(a) for a in acc])
+    def spread(value, buf, send, recv, offsets, slot):
+        buf[slot] = value
+        copies = []
+        for k, offset in enumerate(offsets):
+            c = pltpu.make_async_remote_copy(
+                src_ref=buf.at[slot], dst_ref=buf.at[slot], send_sem=send.at[k],
+                recv_sem=recv.at[k], device_id=at(offset), device_id_type=MESH,
+            )
+            c.start()
+            copies.append(c)
+        return copies
+
+    def stacked(acc):
+        parts = [jnp.sum(a, axis=0, keepdims=True) for a in acc]
+        return jnp.concatenate(parts + [jnp.zeros((ROWS - 4, LANES), F32)], axis=0)
+
+    def gathered(copies, buf):
+        for c in copies:
+            c.wait_recv()
+        total = buf[0]
+        for k in range(1, buf.shape[0]):
+            total = total + buf[k]
+        return total
+
+    def solve(total):
+        total = jnp.sum(total, axis=1, keepdims=True)
+        return coefficients(*[total[k : k + 1] for k in range(4)])
+
+    acc = lax.fori_loop(PAD, PAD + xc, coarse_moments, (zero,) * 4, unroll=2)
+    coarse_copies = spread(
+        stacked(acc), ac, sc, rc, [(d, 0, 0) for d in range(1, nx)], ix
+    )
+
+    arrive(z_fine)
+    halo_fine = x_swap(fb, of, xf, yf, 2, bf[0])
+    halo_fine += y_swap(fb, of, xf, yf, 2, 2, f_up, f_dn, f_fu, f_fd, of_l, of_r, bf[0])
+    start(halo_fine)
+    mid_lanes = lane_prolong(zm, 0, 0, zm, zc)
+    mid_rows = row_prolong(ym, ROWS, iy, ym * ny, yc, yc, 0, 0)
+    ka, kb = solve(gathered(coarse_copies, ac))
     for j in range(xc + 6):
-        cx[j] = ka * cr[ix * xc + j] + kb * cw[ix * xc + j]
+        cx[j] = ka * cr[j + 1] + kb * cw[j + 1]
     out_c[...] = cx[3 : 3 + xc]
 
     def prolong(src, tz, dst, lane_matrix, row_matrix):
@@ -359,7 +400,7 @@
             r[p] = value * (mask * inside(p))
             return carry
 
-        lax.fori_loop(PAD - reach, PAD + own + reach, make_r, 0)
+        lax.fori_loop(PAD - reach, PAD + own + reach, make_r, 0, unroll=4)
 
         def make_w(p, carry):
             c = r[p]
@@ -367,7 +408,7 @@
             w[p] = value * (mask * inside(p))
             return carry
 
-        lax.fori_loop(PAD - reach + 1, PAD + own + reach - 1, make_w, 0)
+        lax.fori_loop(PAD - reach + 1, PAD + own + reach - 1, make_w, 0, unroll=4)
 
         def moments(p, acc):
             rv, wv = r[p, 0:rows, 0:lanes], w[p, 0:rows, 0:lanes]
@@ -379,34 +420,12 @@
                 a + fold_rows(v) for a, v in zip(acc, (rv * rv, rv * wv, wv * wv, wv * image))
             )
 
-        return lax.fori_loop(PAD, PAD + own, moments, (zero,) * 4)
-
-    def exchange(acc, buf, send, recv, offsets, slot):
-        parts = [jnp.sum(a, axis=0, keepdims=True) for a in acc]
-        buf[slot] = jnp.concatenate(parts + [jnp.zeros((ROWS - 4, LANES), F32)], axis=0)
-        copies = []
-        for k, offset in enumerate(offsets):
-            c = pltpu.make_async_remote_copy(
-                src_ref=buf.at[slot], dst_ref=buf.at[slot], send_sem=send.at[k],
-                recv_sem=recv.at[k], device_id=at(offset), device_id_type=MESH,
-            )
-            c.start()
-            copies.append(c)
-        for c in copies:
-            c.wait_recv()
-        total = buf[0]
-        for k in range(1, buf.shape[0]):
-            total = total + buf[k]
-        total = jnp.sum(total, axis=1, keepdims=True)
-        return coefficients(*[total[k : k + 1] for k in range(4)]), copies
-
-    prolong(
-        cx, ctz, ct, lane_prolong(zm, 0, 0, zm, zc),
-        row_prolong(ym, ROWS, iy, ym * ny, yc, yc, 0, 0),
-    )
+        return lax.fori_loop(PAD, PAD + own, moments, (zero,) * 4, unroll=4)
+
+    prolong(cx, ctz, ct, mid_lanes, mid_rows)
     interpolate(ct, mg, xm, -3, xm * nx)
-    arrive(y_mid)
-    left(x_mid)
+    arrive(halo_mid)
+    left(halo_mid)
     y_merge(mb, ym, 4, m_fu, m_fd, mid_planes)
     lanes_m = (iota((LANES, zm), 0) == lax.div(iota((LANES, zm), 1), zm // bm[2])).astype(BF16)
     screens(ms, [om, om_l, om_r], ym, ROWS, bm[1], lanes_m, 1)
@@ -415,21 +434,10 @@
     mask_m = jnp.logical_and(row_m >= 0, row_m < ym * ny).astype(F32)
     ends_m = (iota(shape_m, 1) == 0, iota(shape_m, 1) == zm - 1)
     acc = run_depth(mb, mg, mr, mw, ms, xm, ym, zm, 3, xm // bm[0], ends_m, mask_m)
-    flat = [o for o in peers if o[2] == 0]
-    (ka, kb), mid_copies = exchange(acc, am, sm, rm, flat, ix * ny + iy)
-    for p in range(2, xm + 6):
-        value = mg[p] + ka * mr[p] + kb * mw[p]
-        mx[p - 2] = value
-        if PAD <= p < PAD + xm:
-            out_m[p - PAD] = value[0:ym]
-
-    prolong(
-        mx, mtz, mt, lane_prolong(zf, LANES, iz, zf * nz, zm),
-        row_prolong(yf, ROWS, iy, yf * ny, ym + ROWS, ym, ROWS, iy),
-    )
-    interpolate(mt, fg, xf, -2, xf * nx)
-    arrive(y_fine)
-    left(x_fine)
+    mid_copies = spread(stacked(acc), am, sm, rm, flat, ix * ny + iy)
+
+    arrive(halo_fine)
+    left(halo_fine)
     left(z_fine)
     y_merge(fb, yf, 2, f_fu, f_fd, fine_planes)
     shape_e = (2 * LANES, zf + LANES)
@@ -447,8 +455,22 @@
     mask_f = jnp.logical_and(
         jnp.logical_and(row_f >= 0, row_f < yf * ny), jnp.logical_and(lane_f >= 0, lane_f < zf * nz)
     ).astype(F32)
+    fine_lanes = lane_prolong(zf, LANES, iz, zf * nz, zm)
+    fine_rows = row_prolong(yf, ROWS, iy, yf * ny, ym + ROWS, ym, ROWS, iy)
+    ka, kb = solve(gathered(mid_copies, am))
+    for p in range(2, xm + 6):
+        value = mg[p] + ka * mr[p] + kb * mw[p]
+        mx[p - 2] = value
+        if PAD <= p < PAD + xm:
+            out_m[p - PAD] = value[0:ym]
+
+    prolong(mx, mtz, mt, fine_lanes, fine_rows)
+    interpolate(mt, fg, xf, -2, xf * nx)
     acc = run_depth(fb, fg, fr, fw, fs, xf, yf, zf, 2, xf // bf[0], (None, None), mask_f)
-    (ka, kb), fine_copies = exchange(acc, af, sf, rf, peers, (ix * ny + iy) * nz + iz)
+    fine_copies = spread(stacked(acc), af, sf, rf, flat, ix * ny + iy)
+    total = gathered(fine_copies, af)
+    last_copies = spread(total, ag, sg, rg, across, iz)
+    ka, kb = solve(gathered(last_copies, ag))
 
     def finish(x, carry):
         p = x + PAD
@@ -457,18 +479,11 @@
         )
         return carry
 
-    lax.fori_loop(0, xf, finish, 0)
-
-    for _, c, _ in gather:
+    lax.fori_loop(0, xf, finish, 0, unroll=4)
+
+    left(x_coarse)
+    for c in coarse_copies + mid_copies + fine_copies + last_copies:
         c.wait_send()
-    left(not_in(sends, x_mid + x_fine + z_fine))
-    for c in mid_copies + fine_copies:
-        c.wait_send()
-
-
-def not_in(items, waited):
-    done = [id(item) for item in waited]
-    return [item for item in items if id(item) not in done]
 
 
 def shards(dims, *args):
@@ -484,9 +499,9 @@
 
     bm, bf = occ_m.shape[0] + 2, occ_f.shape[0] + 2
     scratch = [
-        buf(xc * nx + 6, yc, zc), buf(xc * nx + 6, yc, zc), buf(occ_c.shape[0] * nx, yc, zc),
+        buf(xc + 8, yc, zc), buf(xc + 8, yc, zc), buf(occ_c.shape[0] + 2, yc, zc),
         buf(xc + 6, yc, zc), buf(xc + 6, yc, zm), buf(xc + 6, *me),
-        buf(occ_c.shape[0] * nx, ROWS, LANES),
+        buf(occ_c.shape[0] + 2, ROWS, LANES),
         buf(xm + 8, *me), buf(xm + 8, *me), buf(xm + 8, *me), buf(xm + 8, *me), buf(bm, *me),
         buf(xm + 4, *me), buf(xm + 4, me[0], fe[1]), buf(xm + 4, *fe),
         buf(bm, ROWS, LANES),
@@ -496,15 +511,15 @@
         buf(bf, ROWS, 2 * LANES),
         buf(xf + 4, 2, fe[1]), buf(xf + 4, 2, fe[1]), buf(xf + 4, 2, fe[1]), buf(xf + 4, 2, fe[1]),
         buf(bf, ROWS, 2 * LANES), buf(bf, ROWS, 2 * LANES),
-        buf(nx * ny, ROWS, LANES), buf(nx * ny * nz, ROWS, LANES),
-        pltpu.SemaphoreType.DMA((2 * nx + 16,)), pltpu.SemaphoreType.DMA((2 * nx + 16,)),
-        pltpu.SemaphoreType.DMA((nx * ny,)), pltpu.SemaphoreType.DMA((nx * ny,)),
-        pltpu.SemaphoreType.DMA((nx * ny * nz,)), pltpu.SemaphoreType.DMA((nx * ny * nz,)),
+        buf(nx, ROWS, LANES), buf(nx * ny, ROWS, LANES), buf(nx * ny, ROWS, LANES),
+        buf(nz, ROWS, LANES),
     ]
+    for count in (40, nx, nx * ny, nx * ny, nz):
+        scratch += [pltpu.SemaphoreType.DMA((count,))] * 2
     vmem = pl.BlockSpec(memory_space=pltpu.VMEM)
     return pl.pallas_call(
         functools.partial(kernel, dims),
-        out_shape=[jax.ShapeDtypeStruct(a.shape, F32) for a in args[:3]],
+        out_shape=[pltpu.VMEM(a.shape, F32) for a in args[:3]],
         in_specs=[vmem] * 6 + [pl.BlockSpec(memory_space=pltpu.SMEM)],
         out_specs=[vmem] * 3,
         scratch_shapes=scratch,

time: 63.7 us -> 41.9 us (0.66)
  Pallas kernels: 58.2 us -> 38.3 us
  local copies, waits for them, and re-layouts: 4.62 us -> 2.33 us
    pallas_call x1, Pallas kernels: 58.2 us -> 38.3 us  [shards(): pl.pallas_call(functools.partial(kernel, dims), out_shape=[pltpu.VMEM(a.s...]
    unnamed x5 -> x3, local copies, waits for them, and re-layouts: 4.62 us -> 2.33 us
where the time goes in v2:
time: 41.9 us; the launch traced here: 41.3 us
  Pallas kernels  38.3 us (91%)
  local copies, waits for them, and re-layouts  2.33 us (6%)
  between operations  0.64 us (2%)
    pallas_call x1, Pallas kernels, shards(): pl.pallas_call(functools.partial(kernel, dims), out_shape=[pltpu.VMEM(a.s...  38.3 us
    unnamed x3, local copies, waits for them, and re-layouts  2.33 us

profile of v2, /device:TPU:0, one launch (start us, length us, event | category | flops | bytes accessed | tf_op | source)
XLA Modules:
  0.0 41.3 jit_solution(12695069832197165470)
XLA Ops:
  0.6 38.3 %shard_map.94 = (f32[8,32,128]{2,1,0:T(8,128)S(1)}, f32[16,16,256]{2,1,0:T(8,128)S(1)}, f32[32,32,256]{2,1,0:T(8,128)S(1)}) custom-call(bf16[8,32,128]{2,1,0:T(8,128)(2,1)} %rhs_c.1, bf16[16,16,256]{2,1,0:T(8,128)(2,1)} %rhs_m.1, bf16[32,32,256]{2,1,0:T(8,128)(2,1)} %rhs_f.1, s32[1,4,16]{2,1,0:T(4,128)} %occ_c.1, s32[2,2,32]{2,1,0:T(2,128)} %occ_m.1, ...), custom_call_target="tpu_custom_call" | custom-call | tf_op jit(solution)/shard_map/pallas_call | solution.py:520
  39.0 0.7 %copy.13 = f32[8,32,128]{2,1,0:T(8,128)} copy(f32[8,32,128]{2,1,0:T(8,128)S(1)} %get-tuple-element.3) | data formatting | bytes 262144
  39.6 0.7 %copy.14 = f32[16,16,256]{2,1,0:T(8,128)} copy(f32[16,16,256]{2,1,0:T(8,128)S(1)} %get-tuple-element.4) | data formatting | bytes 524288
  40.3 1.0 %copy.15 = f32[32,32,256]{2,1,0:T(8,128)} copy(f32[32,32,256]{2,1,0:T(8,128)S(1)} %get-tuple-element.5) | data formatting | bytes 2097152

commit v3 on v2

--- a/solution.py
+++ b/solution.py
@@ -297,7 +297,7 @@
         cw[p] = keep * (screen * r - (cr[p - 1] + cr[p + 1] + sum_c(r, True)))
         return carry
 
-    lax.fori_loop(1, xc + 7, coarse_w, 0, unroll=2)
+    lax.fori_loop(1, xc + 7, coarse_w, 0, unroll=7)
 
     def coarse_moments(p, acc):
         r, w = cr[p], cw[p]
@@ -335,7 +335,7 @@
         total = jnp.sum(total, axis=1, keepdims=True)
         return coefficients(*[total[k : k + 1] for k in range(4)])
 
-    acc = lax.fori_loop(PAD, PAD + xc, coarse_moments, (zero,) * 4, unroll=2)
+    acc = lax.fori_loop(PAD, PAD + xc, coarse_moments, (zero,) * 4, unroll=4)
     coarse_copies = spread(
         stacked(acc), ac, sc, rc, [(d, 0, 0) for d in range(1, nx)], ix
     )
@@ -400,7 +400,7 @@
             r[p] = value * (mask * inside(p))
             return carry
 
-        lax.fori_loop(PAD - reach, PAD + own + reach, make_r, 0, unroll=4)
+        lax.fori_loop(PAD - reach, PAD + own + reach, make_r, 0, unroll=6)
 
         def make_w(p, carry):
             c = r[p]
@@ -408,7 +408,7 @@
             w[p] = value * (mask * inside(p))
             return carry
 
-        lax.fori_loop(PAD - reach + 1, PAD + own + reach - 1, make_w, 0, unroll=4)
+        lax.fori_loop(PAD - reach + 1, PAD + own + 1 + (reach - 2), make_w, 0, unroll=6)
 
         def moments(p, acc):
             rv, wv = r[p, 0:rows, 0:lanes], w[p, 0:rows, 0:lanes]
@@ -420,7 +420,7 @@
                 a + fold_rows(v) for a, v in zip(acc, (rv * rv, rv * wv, wv * wv, wv * image))
             )
 
-        return lax.fori_loop(PAD, PAD + own, moments, (zero,) * 4, unroll=4)
+        return lax.fori_loop(PAD, PAD + own, moments, (zero,) * 4, unroll=8)
 
     prolong(cx, ctz, ct, mid_lanes, mid_rows)
     interpolate(ct, mg, xm, -3, xm * nx)

time: 41.9 us -> 41.3 us (0.986)
  Pallas kernels: 38.3 us -> 37.8 us
    pallas_call x1, Pallas kernels: 38.3 us -> 37.8 us  [shards(): pl.pallas_call(functools.partial(kernel, dims), out_shape=[pltpu.VMEM(a.s...]
where the time goes in v3:
time: 41.3 us; the launch traced here: 40.7 us
  Pallas kernels  37.8 us (92%)
  local copies, waits for them, and re-layouts  2.33 us (6%)
  between operations  0.64 us (2%)
    pallas_call x1, Pallas kernels, shards(): pl.pallas_call(functools.partial(kernel, dims), out_shape=[pltpu.VMEM(a.s...  37.8 us
    unnamed x3, local copies, waits for them, and re-layouts  2.33 us

profile of v3, /device:TPU:0, one launch (start us, length us, event | category | flops | bytes accessed | tf_op | source)
XLA Modules:
  0.0 40.7 jit_solution(8359447661493429291)
XLA Ops:
  0.6 37.8 %shard_map.94 = (f32[8,32,128]{2,1,0:T(8,128)S(1)}, f32[16,16,256]{2,1,0:T(8,128)S(1)}, f32[32,32,256]{2,1,0:T(8,128)S(1)}) custom-call(bf16[8,32,128]{2,1,0:T(8,128)(2,1)} %rhs_c.1, bf16[16,16,256]{2,1,0:T(8,128)(2,1)} %rhs_m.1, bf16[32,32,256]{2,1,0:T(8,128)(2,1)} %rhs_f.1, s32[1,4,16]{2,1,0:T(4,128)} %occ_c.1, s32[2,2,32]{2,1,0:T(2,128)} %occ_m.1, ...), custom_call_target="tpu_custom_call" | custom-call | tf_op jit(solution)/shard_map/pallas_call | solution.py:520
  38.4 0.7 %copy.13 = f32[8,32,128]{2,1,0:T(8,128)} copy(f32[8,32,128]{2,1,0:T(8,128)S(1)} %get-tuple-element.3) | data formatting | bytes 262144
  39.1 0.7 %copy.14 = f32[16,16,256]{2,1,0:T(8,128)} copy(f32[16,16,256]{2,1,0:T(8,128)S(1)} %get-tuple-element.4) | data formatting | bytes 524288
  39.8 1.0 %copy.15 = f32[32,32,256]{2,1,0:T(8,128)} copy(f32[32,32,256]{2,1,0:T(8,128)S(1)} %get-tuple-element.5) | data formatting | bytes 2097152
